TPU v7x, 512 devices: a whole 4x8x8 slice. The times are simulated.
512 devices in a mesh: slab: 512 (over z, x, y, core).
Axes of the slice: x: 4, y: 8, z: 8, core: 2. Of those that a mesh axis runs over, the one named last changes fastest.
Arguments:
- start_vectors: float32 [2, 512, 256, 256], P(None, 'slab'), may hold values from -6 to 6
- levels: int32 [512, 256, 256], P('slab'), may hold values from 0 to 15
- energies: float32 [16], replicated, may hold values from -4 to 4
Outputs:
- cheb_field: float32 [2, 512, 256, 256], P(None, 'slab')
- lanczos_diag: float32 [2, 8], replicated
- lanczos_off: float32 [2, 7], replicated
- moments: float32 [2, 6], replicated
All inputs are finite; a program needn't handle non-finite values.
Results may differ from a plain program's by a relative error of at most 0.0001.
Values sent between devices are 32-bit elements; how exact they have to be, the bound alone decides.
A program may use at most 64 MiB of HBM per device.

v0:
```python
import functools

import jax
import jax.numpy as jnp
from jax import lax
from jax.experimental import pallas as pl
from jax.experimental.pallas import tpu as pltpu
from jax.sharding import PartitionSpec as P

LANCZOS = 8
HALF = LANCZOS // 2
GROUP = 8
GHOST = 8
RETURNED = 3


def phase_one(dots, half, sqrt):
    norm = dots[0]
    nu = [None] * len(dots)
    nu[0] = norm / norm
    nu[1] = dots[1] / norm
    for k in range(2, len(dots)):
        nu[k] = 2.0 * dots[k] / norm - nu[k % 2]
    top = len(nu) - 1
    row, before = list(nu), None
    diag, offd = [], []
    for k in range(half):
        if k == 0:
            alpha = row[1]
        else:
            alpha = (0.5 * row[k + 1] - offd[-1] * before[k]) / row[k]
        diag.append(alpha)
        new = [None] * len(nu)
        for l in range(k + 1, top - k):
            new[l] = 0.5 * (row[l + 1] + row[l - 1]) - alpha * row[l]
            if k:
                new[l] = new[l] - offd[-1] * before[l]
        beta = sqrt(new[k + 1] / (row[k] if k == 0 else 2.0 * row[k]))
        offd.append(beta)
        inv = 1.0 / beta
        before, row = row, [None if x is None else x * inv for x in new]
    zero = nu[0] * 0.0
    scale = 1.0 / sqrt(norm)
    vectors = [[scale] + [zero] * half]
    for k in range(half):
        now = vectors[-1]
        inv = 1.0 / offd[k]
        shifted = [zero] * (half + 1)
        for l in range(k + 1):
            if l == 0:
                shifted[1] = shifted[1] + now[0]
            else:
                shifted[l + 1] = shifted[l + 1] + 0.5 * now[l]
                shifted[l - 1] = shifted[l - 1] + 0.5 * now[l]
        new = [shifted[l] - diag[k] * now[l] for l in range(half + 1)]
        if k:
            new = [x - offd[k - 1] * y for x, y in zip(new, vectors[-2])]
        vectors.append([x * inv for x in new])
    return nu, diag, offd, vectors


def phase_two(dots, diag, offd, half, sqrt):
    count = len(dots)
    gram = {}
    for k, value in enumerate(dots):
        gram[(half + k // 2, half + (k + 1) // 2)] = value
    zero = dots[0] * 0.0
    one = zero + 1.0
    for k in range(half):
        gram[(k, half)] = zero
        gram[(k, half - 1)] = one if k == half - 1 else zero
    guess_a, guess_b = diag[half - 1], offd[half - 1]
    inv = 1.0 / guess_b

    def entry(i, j):
        if (i, j) in gram:
            return gram[(i, j)]
        if j > half and i < half and (j - half) < (half - i) + 1:
            value = zero
        elif i >= half:
            value = entry(i + 1, j - 1) + entry(i - 1, j - 1) - entry(i, j - 2)
        else:
            value = (offd[i] * inv) * entry(i + 1, j - 1) - entry(i, j - 2)
            if i != half - 1:
                value = value + ((diag[i] - guess_a) * inv) * entry(i, j - 1)
            if i > 0:
                value = value + (offd[i - 1] * inv) * entry(i - 1, j - 1)
        gram[(i, j)] = value
        return value

    top = half + count - 1
    row = {l: entry(half, l) for l in range(half, top + 1)}
    before = {l: entry(half - 1, l) for l in range(half, top)}
    diag, offd = list(diag), list(offd)
    for k in range(half, 2 * half):
        if k == half:
            alpha = guess_a + guess_b * row[k + 1] / row[k]
        else:
            alpha = guess_a + (guess_b * row[k + 1] - offd[k - 1] * before[k]) / row[k]
        diag.append(alpha)
        if k == 2 * half - 1:
            break
        new = {}
        for l in range(k + 1, top - (k - half)):
            new[l] = guess_b * (row[l + 1] + row[l - 1]) + (guess_a - alpha) * row[l] - offd[k - 1] * before[l]
        beta = sqrt(new[k + 1] * guess_b / row[k])
        offd.append(beta)
        inv_b = 1.0 / beta
        before, row = row, {l: x * inv_b for l, x in new.items()}
    return diag, offd


def chebyshev(diag, offd, nu, centre, width):
    left = [None] + offd
    right = offd + [None]
    low, high = None, None
    for a, b, c in zip(diag, left, right):
        reach = b if c is None else c if b is None else b + c
        low = a - reach if low is None else jnp.minimum(low, a - reach)
        high = a + reach if high is None else jnp.maximum(high, a + reach)
    inv = 1.0 / (0.55 * (high - low))
    al = width * inv
    be = (centre - 0.5 * (high + low)) * inv
    p, q, r = 2.0 * be * be + al * al - 1.0, 4.0 * al * be, al * al
    first = [be, al]
    second = [p, q, r]
    third = [2.0 * be * p + al * q - be, 2.0 * be * q + al * (2.0 * p + r) - al, 2.0 * be * r + al * q, al * r]

    def dot(f, g):
        total = None
        for i, x in enumerate(f):
            for j, y in enumerate(g):
                term = (x * y) * (0.5 * (nu[i + j] + nu[abs(i - j)]))
                total = term if total is None else total + term
        return total

    start = [nu[0]]
    m1 = dot(start, first)
    moments = [
        m1,
        dot(start, second),
        dot(start, third),
        2.0 * dot(second, second) - 1.0,
        2.0 * dot(third, second) - m1,
        2.0 * dot(third, third) - 1.0,
    ]
    return third, moments


def kernel(
    count, energies, start, levels, cheb, diag_out, offd_out, moments_out,
    own, own_levels, field, halo, onsite, level, back, part, part_far, mine,
    load_sem, vec_sem, level_sem, halo_send, halo_recv, back_send, back_recv, red_send, red_recv,
):
    me = lax.axis_index("slab")
    member = lax.rem(me, GROUP)
    group = me // GROUP
    base = me - member
    groups = count // GROUP
    vecs, _, height, lanes = start.shape
    my_vec, block = lax.rem(member, vecs), member // vecs
    rows = height // (GROUP // vecs)
    deep = rows + 2 * GHOST
    mesh_id = pl.DeviceIdType.MESH
    ahead = lax.rem(me + GROUP, count)
    behind = lax.rem(me + count - GROUP, count)

    loads = [
        pltpu.make_async_copy(start.at[:, 0], own, load_sem.at[0]),
        pltpu.make_async_copy(levels.at[0], own_levels, load_sem.at[1]),
    ]
    for copy in loads:
        copy.start()

    def peer(i):
        return base + lax.rem(member + i, GROUP)

    def far(i):
        return lax.rem(me + i * GROUP, count)

    barrier = pltpu.get_barrier_semaphore()

    def greet(i, carry):
        pl.semaphore_signal(barrier, inc=1, device_id=(peer(i),), device_id_type=mesh_id)
        return carry

    def greet_far(i, carry):
        pl.semaphore_signal(barrier, inc=1, device_id=(far(i),), device_id_type=mesh_id)
        return carry

    lax.fori_loop(1, GROUP, greet, 0)
    lax.fori_loop(1, groups, greet_far, 0)
    pl.semaphore_wait(barrier, GROUP - 1 + groups - 1)

    def pieces(i):
        i = i // vecs
        mid = pl.multiple_of(i * rows, 8)
        top = pl.multiple_of(lax.rem(i * rows + height - GHOST, height), 8)
        low = pl.multiple_of(lax.rem(i * rows + rows, height), 8)
        return ((mid, GHOST, rows), (top, 0, GHOST), (low, GHOST + rows, GHOST))

    def vec_refs(i):
        return [
            (own.at[lax.rem(i, vecs), pl.ds(at, size)], field.at[0, member, pl.ds(to, size)])
            for at, to, size in pieces(i)
        ]

    def level_refs(i):
        return [
            (own_levels.at[pl.ds(at, size)], level.at[member, pl.ds(to, size)])
            for at, to, size in pieces(i)
        ]

    def scatter(refs, sems):
        def body(i, carry):
            to = lax.rem(member + i, GROUP)
            for src, dst in refs(to):
                pltpu.make_async_remote_copy(
                    src_ref=src, dst_ref=dst, send_sem=sems.at[0], recv_sem=sems.at[1],
                    device_id=(base + to,), device_id_type=mesh_id,
                ).start()
            return carry

        lax.fori_loop(1, GROUP, body, 0)
        for src, dst in refs(member):
            pltpu.make_async_copy(src, dst, sems.at[1]).start()

    def drain(ref, sem):
        pltpu.make_async_copy(ref, ref, sem).wait()

    loads[0].wait()
    scatter(vec_refs, vec_sem)
    loads[1].wait()
    scatter(level_refs, level_sem)

    values = [energies[i] for i in range(energies.shape[0])]
    mean = sum(values[1:], values[0]) * (1.0 / len(values))
    spread = [(x - mean) * (x - mean) for x in values]
    spread = sum(spread[1:], spread[0]) * (1.0 / len(values))
    width = 2.0 * jnp.sqrt(jnp.full((1, lanes), spread + 6.0, jnp.float32))
    inv_width = 1.0 / width

    def halo_copies(slot, at):
        part_of = pl.ds(GHOST, rows) if at == LANCZOS - 1 else pl.ds(0, deep)
        return [
            pltpu.make_async_remote_copy(
                src_ref=field.at[slot, plane, part_of], dst_ref=halo.at[at, side, part_of],
                send_sem=halo_send.at[at, side], recv_sem=halo_recv.at[at, side],
                device_id=(to,), device_id_type=mesh_id,
            )
            for plane, side, to in ((0, 1, behind), (GROUP - 1, 0, ahead))
        ]

    def give_back(k):
        def refs(i):
            return (
                field.at[k, i, pl.ds(GHOST, rows)],
                back.at[k - 1, my_vec, pl.ds(pl.multiple_of(block * rows, 8), rows)],
            )

        def body(i, carry):
            to = lax.rem(member + i, GROUP)
            src, dst = refs(to)
            pltpu.make_async_remote_copy(
                src_ref=src, dst_ref=dst, send_sem=back_send.at[k - 1], recv_sem=back_recv.at[k - 1],
                device_id=(base + to,), device_id_type=mesh_id,
            ).start()
            return carry

        lax.fori_loop(1, GROUP, body, 0)
        src, dst = refs(member)
        pltpu.make_async_copy(src, dst, back_recv.at[k - 1]).start()

    def tile_sum(x):
        x = x[GHOST : GHOST + rows]
        total = x[0:8]
        for i in range(8, rows, 8):
            total = total + x[i : i + 8]
        return total

    def step(source, target, before, at, combine, awaited, extra=False):
        nothing = jnp.zeros((8, lanes), jnp.float32)

        def local(m, here, *beside):
            near = pltpu.roll(here, 1, 0) + pltpu.roll(here, deep - 1, 0)
            near = near + pltpu.roll(here, 1, 1) + pltpu.roll(here, lanes - 1, 1)
            for plane in beside:
                near = near + field[source, plane]
            return onsite[m] * here - inv_width * near

        def finish(m, here, applied):
            new = combine(applied, here, None if before is None else field[before, m])
            if target is not None:
                field[target, m] = new
            return new

        def add(sums, here, new):
            sums = list(sums)
            sums[0] = sums[0] + tile_sum(here * new)
            sums[1] = sums[1] + tile_sum(new * new)
            if extra:
                sums[2] = sums[2] + tile_sum(here * here)
            return tuple(sums)

        def plane(m, sums):
            here = field[source, m]
            return add(sums, here, finish(m, here, local(m, here, m - 1, m + 1)))

        faces = ((0, 1), (GROUP - 1, GROUP - 2))
        parts = [local(m, field[source, m], inner) for m, inner in faces]
        for copy in awaited:
            copy.wait_recv()
        news = [
            finish(m, field[source, m], part - inv_width * halo[at, side])
            for side, ((m, inner), part) in enumerate(zip(faces, parts))
        ]
        sent = []
        if target is not None:
            sent = halo_copies(target, at + 1)
            for copy in sent:
                copy.start()
        sums = (nothing,) * 3
        for (m, inner), new in zip(faces, news):
            sums = add(sums, field[source, m], new)
        sums = lax.fori_loop(
            1,
            GROUP - 1,
            plane,
            sums,
            unroll=3,
        )
        return sums, sent

    lane = lax.broadcasted_iota(jnp.int32, (8, 128), 1)
    line = lax.broadcasted_iota(jnp.int32, (8, 128), 0)

    def reduce_all(dots, turn):
        tile = jnp.zeros((8, 128), jnp.float32)
        for d, value in enumerate(dots):
            whole = jnp.sum(jnp.sum(value, axis=0, keepdims=True), axis=1, keepdims=True)
            tile = jnp.where((lane == d) & (line == my_vec), whole, tile)
        for leg, (slots, index, size, target) in enumerate(
            ((part.at[turn], member, GROUP, peer), (part_far.at[turn], group, groups, far))
        ):
            mine[turn, leg] = tile
            slots[index] = tile

            def body(i, carry):
                pltpu.make_async_remote_copy(
                    src_ref=mine.at[turn, leg], dst_ref=slots.at[index],
                    send_sem=red_send.at[turn, leg], recv_sem=red_recv.at[turn, leg],
                    device_id=(target(i),), device_id_type=mesh_id,
                ).start()
                return carry

            lax.fori_loop(1, size, body, 0)
            drain(slots.at[pl.ds(0, size - 1)], red_recv.at[turn, leg])
            tile = slots[0]
            for i in range(1, size):
                tile = tile + slots[i]
        return [
            jnp.broadcast_to(tile[0:vecs, d : d + 1], (vecs, lanes)) for d in range(len(dots))
        ]

    drain(field.at[0], vec_sem.at[1])
    sent = [halo_copies(0, 0)]
    for copy in sent[0]:
        copy.start()
    drain(level, level_sem.at[1])

    def look_up(m, carry):
        ids = level[m]
        energy = jnp.full(ids.shape, values[0] - mean, jnp.float32)
        for i in range(1, len(values)):
            energy = jnp.where(ids == i, values[i] - mean, energy)
        onsite[m] = energy * inv_width
        return carry

    lax.fori_loop(0, GROUP, look_up, 0)

    def arrive(copies):
        for copy in copies:
            copy.wait_recv()

    dots = [None]
    for k in range(HALF):
        if k == 0:
            rule = lambda applied, here, old: applied
        else:
            rule = lambda applied, here, old: 2.0 * applied - old
        sums, copies = step(k, k + 1, k - 1 if k else None, k, rule, sent[k], extra=k == 0)
        sent.append(copies)
        if k == 0:
            dots[0] = sums[2]
        dots.append(sums[0])
        dots.append(sums[1])
        if k + 1 <= RETURNED:
            give_back(k + 1)

    totals = reduce_all(dots, 0)
    nu, diag, offd, vectors = phase_one(totals, HALF, jnp.sqrt)
    arrive(sent[HALF])
    old_at, new_at = HALF + 1, HALF + 2

    def mix(coefficients, read):
        total = coefficients[0] * read(0)
        for k in range(1, len(coefficients)):
            total = total + coefficients[k] * read(k)
        return total

    which = jnp.full((1, lanes), my_vec, jnp.int32)

    def pick(value):
        row = value[0:1]
        for v in range(1, vecs):
            row = jnp.where(which == v, value[v : v + 1], row)
        return row

    old_mix = [pick(x) for x in vectors[HALF - 1][:HALF]]
    new_mix = [pick(x) for x in vectors[HALF]]
    for side in range(2):
        halo[HALF, side] = mix(new_mix, lambda k: halo[k, side])

    def restart(m, total):
        field[old_at, m] = mix(old_mix, lambda k: field[k, m])
        new = mix(new_mix, lambda k: field[k, m])
        field[new_at, m] = new
        return total + tile_sum(new * new)

    dots = [
        lax.fori_loop(0, GROUP, restart, jnp.zeros((8, lanes), jnp.float32), unroll=2)
    ]
    gain = pick(1.0 / offd[HALF - 1])
    shift = pick(diag[HALF - 1])

    def rule(applied, here, old):
        return gain * (applied - shift * here) - old

    for k in range(HALF):
        at = HALF + k
        last = k == HALF - 1
        sums, copies = step(new_at + k, None if last else new_at + k + 1, new_at + k - 1, at, rule, sent[at] if k else [])
        sent.append(copies)
        dots.append(sums[0])
        if not last:
            dots.append(sums[1])

    totals = reduce_all(dots, 1)
    diag, offd = phase_two(totals, diag, offd, HALF, jnp.sqrt)
    diag = [width * a + mean for a in diag]
    offd = [width * b for b in offd]
    third, moments = chebyshev(diag, offd, nu, mean, width)

    for k in range(RETURNED):
        drain(back.at[k], back_recv.at[k])
    for v in range(vecs):
        cheb[v, 0] = mix([x[v : v + 1] for x in third], lambda k: own[v] if k == 0 else back[k - 1, v])

    for ref, items in ((diag_out, diag), (offd_out, offd), (moments_out, moments)):
        at = lax.broadcasted_iota(jnp.int32, ref.shape, 1)
        value = jnp.zeros(ref.shape, jnp.float32)
        for i, item in enumerate(items):
            value = jnp.where(at == i, item[:, : ref.shape[1]], value)
        ref[...] = value

    for copies in sent:
        for copy in copies:
            copy.wait_send()
    drain(field.at[0, pl.ds(0, GROUP - 1)], vec_sem.at[0])
    drain(level.at[pl.ds(0, GROUP - 1)], level_sem.at[0])
    for k in range(RETURNED):
        drain(field.at[k + 1, pl.ds(0, GROUP - 1), pl.ds(GHOST, rows)], back_send.at[k])
    for turn in range(2):
        drain(part.at[turn, pl.ds(0, GROUP - 1)], red_send.at[turn, 0])
        drain(part_far.at[turn, pl.ds(0, groups - 1)], red_send.at[turn, 1])


def shards(count, start_vectors, levels, energies):
    vecs, _, height, lanes = start_vectors.shape
    groups = count // GROUP
    deep = height // (GROUP // vecs) + 2 * GHOST
    f32 = jnp.float32
    vmem = pl.BlockSpec(memory_space=pltpu.VMEM)
    anywhere = pl.BlockSpec(memory_space=pl.ANY)
    dma = pltpu.SemaphoreType.DMA
    return pl.pallas_call(
        functools.partial(kernel, count),
        out_shape=(
            jax.ShapeDtypeStruct(start_vectors.shape, f32),
            jax.ShapeDtypeStruct((vecs, LANCZOS), f32),
            jax.ShapeDtypeStruct((vecs, LANCZOS - 1), f32),
            jax.ShapeDtypeStruct((vecs, 6), f32),
        ),
        in_specs=[pl.BlockSpec(memory_space=pltpu.SMEM), anywhere, anywhere],
        out_specs=(vmem,) * 4,
        scratch_shapes=[
            pltpu.VMEM((vecs, height, lanes), f32),
            pltpu.VMEM((height, lanes), jnp.int32),
            pltpu.VMEM((LANCZOS + 2, GROUP, deep, lanes), f32),
            pltpu.VMEM((LANCZOS, 2, deep, lanes), f32),
            pltpu.VMEM((GROUP, deep, lanes), f32),
            pltpu.VMEM((GROUP, deep, lanes), jnp.int32),
            pltpu.VMEM((RETURNED, vecs, height, lanes), f32),
            pltpu.VMEM((2, GROUP, 8, 128), f32),
            pltpu.VMEM((2, groups, 8, 128), f32),
            pltpu.VMEM((2, 2, 8, 128), f32),
            dma((2,)),
            dma((2,)),
            dma((2,)),
            dma((LANCZOS, 2)),
            dma((LANCZOS, 2)),
            dma((RETURNED,)),
            dma((RETURNED,)),
            dma((2, 2)),
            dma((2, 2)),
        ],
        compiler_params=pltpu.CompilerParams(
            collective_id=0, has_side_effects=True, vmem_limit_bytes=67043328
        ),
    )(energies, start_vectors, levels)


def solution(mesh):
    in_specs = (P(None, "slab", None, None), P("slab", None, None), P())
    out_specs = (P(None, "slab", None, None), P(), P(), P())
    return jax.shard_map(
        functools.partial(shards, mesh.shape["slab"]),
        mesh=mesh, in_specs=in_specs, out_specs=out_specs, check_vma=False,
    )
```

profile of v0, /device:TPU:1, one launch (start us, length us, event | category | flops | bytes accessed | tf_op | source)
XLA Modules:
  0.0 187.8 jit_solution(10046386326785671474)
XLA Ops:
  0.6 183.4 %shard_map.66 = (f32[2,1,256,256]{3,2,1,0:T(8,128)}, f32[2,8]{1,0:T(2,128)}, f32[2,7]{1,0:T(2,128)}, f32[2,6]{1,0:T(2,128)}) custom-call(f32[16]{0:T(128)} %energies.1, f32[2,1,256,256]{3,2,1,0:T(8,128)} %start.1, s32[1,256,256]{2,1,0:T(8,128)} %levels.1), custom_call_target="tpu_custom_call" | custom-call | tf_op jit(solution)/shard_map/pallas_call | solution.py:486
  184.0 0.0 copy-start.2
  184.0 1.9 copy.11
  185.9 0.0 copy-done.2
  185.9 0.0 copy-start.1
  185.9 0.6 copy.12
  186.4 0.1 copy-done.1
  186.5 0.0 copy-start
  186.5 0.6 copy.13
  187.1 0.1 copy-done
  187.2 0.6 copy.14
Async XLA Ops:
  184.0 1.9 %copy-start.2 = (f32[2,8]{1,0:T(2,128)S(1)}, f32[2,8]{1,0:T(2,128)}, u32[]{:S(2)}) copy-start(f32[2,8]{1,0:T(2,128)} %get-tuple-element.9) | copy-start | bytes 196
  185.9 0.7 copy-start.1
  186.5 0.7 copy-start
where the time goes:
time: 189 us; the launch traced here: 188 us
  Pallas kernels  183 us (97%)
  local copies, waits for them, and re-layouts  3.76 us (2%)
    pallas_call x1, Pallas kernels, shards(): pl.pallas_call(functools.partial(kernel, count), out_shape=(jax.ShapeDtyp...  183 us

commit v1 on v0

v1 whole, which is shorter than its diff:
```python
import functools

import jax
import jax.numpy as jnp
from jax import lax
from jax.experimental import pallas as pl
from jax.experimental.pallas import tpu as pltpu
from jax.sharding import PartitionSpec as P

LANCZOS = 8
RING = 16
PARTS = 2
PAD = 8
FAR = 64


def two_sum(a, b):
    s = a + b
    t = s - a
    return s, (a - (s - t)) + (b - t)


def quick(a, b):
    s = a + b
    return s, b - (s - a)


def split(a):
    t = 4097.0 * a
    high = t - (t - a)
    return high, a - high


def two_prod(a, b):
    p = a * b
    ah, al = split(a)
    bh, bl = split(b)
    return p, ((ah * bh - p) + ah * bl + al * bh) + al * bl


def add(x, y):
    s, e = two_sum(x[0], y[0])
    return quick(s, e + (x[1] + y[1]))


def sub(x, y):
    return add(x, (-y[0], -y[1]))


def mul(x, y):
    p, e = two_prod(x[0], y[0])
    return quick(p, e + (x[0] * y[1] + x[1] * y[0]))


def scale(x, c):
    return x[0] * c, x[1] * c


def div(x, y):
    q = x[0] / y[0]
    p, e = two_prod(q, y[0])
    return quick(q, (((x[0] - p) - e) + (x[1] - q * y[1])) / y[0])


def coefficients(dots):
    count = len(dots)
    norm = dots[0]
    nu = [(norm[0] / norm[0], norm[0] * 0.0), div(dots[1], norm)]
    for k in range(2, count):
        nu.append(sub(scale(div(dots[k], norm), 2.0), nu[k % 2]))
    row, before = nu, None
    diag, square = [], []
    for k in range(LANCZOS):
        if k == 0:
            alpha = row[1]
        else:
            alpha = div(sub(scale(row[k + 1], 0.5), mul(square[-1], before[k])), row[k])
        diag.append(alpha)
        if k == LANCZOS - 1:
            break
        new = [None] * count
        for l in range(k + 1, count - 1 - k):
            x = sub(scale(add(row[l + 1], row[l - 1]), 0.5), mul(alpha, row[l]))
            new[l] = sub(x, mul(square[-1], before[l])) if k else x
        square.append(div(new[k + 1], row[k] if k == 0 else scale(row[k], 2.0)))
        before, row = row, new
    return [x[0] for x in nu], [x[0] for x in diag], [jnp.sqrt(x[0]) for x in square]


def chebyshev(diag, offd, nu, centre, width):
    left = [None] + offd
    right = offd + [None]
    low, high = None, None
    for a, b, c in zip(diag, left, right):
        reach = b if c is None else c if b is None else b + c
        low = a - reach if low is None else jnp.minimum(low, a - reach)
        high = a + reach if high is None else jnp.maximum(high, a + reach)
    inv = 1.0 / (0.55 * (high - low))
    al = width * inv
    be = (centre - 0.5 * (high + low)) * inv
    p, q, r = 2.0 * be * be + al * al - 1.0, 4.0 * al * be, al * al
    first = [be, al]
    second = [p, q, r]
    third = [2.0 * be * p + al * q - be, 2.0 * be * q + al * (2.0 * p + r) - al, 2.0 * be * r + al * q, al * r]

    def dot(f, g):
        total = None
        for i, x in enumerate(f):
            for j, y in enumerate(g):
                term = (x * y) * (0.5 * (nu[i + j] + nu[abs(i - j)]))
                total = term if total is None else total + term
        return total

    start = [nu[0]]
    m1 = dot(start, first)
    moments = [
        m1,
        dot(start, second),
        dot(start, third),
        2.0 * dot(second, second) - 1.0,
        2.0 * dot(third, second) - m1,
        2.0 * dot(third, third) - 1.0,
    ]
    return third, moments


def kernel(
    count, energies, start, levels, cheb, diag_out, offd_out, moments_out,
    field, halo, level, onsite, near_part, far_part, mine,
    load_sem, send_sem, recv_sem, red_send, red_recv,
):
    me = lax.axis_index("slab")
    member = lax.rem(me, RING)
    ring = me // RING
    base = me - member
    rings = count // RING
    vecs, _, height, lanes = start.shape
    rows = height // PARTS
    mesh_id = pl.DeviceIdType.MESH
    ahead = lax.rem(me + 1, count)
    behind = lax.rem(me + count - 1, count)

    loads = [
        pltpu.make_async_copy(start.at[v, 0], field.at[0, v, pl.ds(PAD, height)], load_sem.at[v]) for v in range(vecs)
    ]
    loads.append(pltpu.make_async_copy(levels.at[0], level, load_sem.at[vecs]))
    for copy in loads:
        copy.start()

    def peer(i):
        return base + lax.rem(member + i, RING)

    def far(i):
        return lax.rem(me + i * RING, count)

    barrier = pltpu.get_barrier_semaphore()

    def greet(to):
        pl.semaphore_signal(barrier, inc=1, device_id=(to,), device_id_type=mesh_id)

    def greet_peer(i, carry):
        greet(peer(i))
        return carry

    def greet_far(i, carry):
        greet(far(i))
        return carry

    greet(ahead)
    greet(behind)
    lax.fori_loop(1, RING, greet_peer, 0)
    lax.fori_loop(1, rings, greet_far, 0)

    values = [energies[i] for i in range(energies.shape[0])]
    mean = sum(values[1:], values[0]) * (1.0 / len(values))
    spread = [(x - mean) * (x - mean) for x in values]
    spread = sum(spread[1:], spread[0]) * (1.0 / len(values))
    width = 2.0 * jnp.sqrt(jnp.full((1, 128), spread + 6.0, jnp.float32))
    inv_width = 1.0 / width
    inv_wide = jnp.concatenate([inv_width] * (lanes // 128), axis=1)

    loads[vecs].wait()
    for at in range(0, height, 64):
        ids = level[at : at + 64]
        energy = jnp.full(ids.shape, values[0] - mean, jnp.float32)
        for i in range(1, len(values)):
            energy = jnp.where(ids == i, values[i] - mean, energy)
        onsite[at : at + 64] = energy * inv_wide

    pl.semaphore_wait(barrier, 2 + RING - 1 + rings - 1)

    def part_copy(k, v, h, side):
        to = ahead if side == 0 else behind
        at = h * rows
        return pltpu.make_async_remote_copy(
            src_ref=field.at[k, v, pl.ds(PAD + at, rows)],
            dst_ref=halo.at[k, side, v, pl.ds(at, rows)],
            send_sem=send_sem.at[k, side, v, h], recv_sem=recv_sem.at[k, side, v, h],
            device_id=(to,), device_id_type=mesh_id,
        )

    def sides(k, h):
        if k < LANCZOS - 1:
            return (0, 1)
        return (0,) if h < PARTS // 2 else (1,)

    sent = []

    def send(k, v, h):
        for side in sides(k, h):
            copy = part_copy(k, v, h, side)
            copy.start()
            sent.append(copy)

    for v in range(vecs):
        loads[v].wait()
        for h in range(PARTS):
            send(0, v, h)
        field[0, v, 0:PAD] = field[0, v, height : height + PAD]
        field[0, v, PAD + height :] = field[0, v, PAD : 2 * PAD]

    def tile_sum(x):
        total = x[0:8]
        for i in range(8, rows, 8):
            total = total + x[i : i + 8]
        return total

    sums = {}

    def note(d, v, x):
        x = tile_sum(x)
        sums[d, v] = sums[d, v] + x if (d, v) in sums else x

    def unit(k, v, h):
        at = h * rows
        big = field[k, v, at : at + rows + 2 * PAD]
        deep = rows + 2 * PAD
        near = (pltpu.roll(big, 1, 0) + pltpu.roll(big, deep - 1, 0))[PAD : PAD + rows]
        here = big[PAD : PAD + rows]
        near = near + pltpu.roll(here, 1, 1) + pltpu.roll(here, lanes - 1, 1)
        for side in sides(k, h):
            part_copy(k, v, h, side).wait_recv()
        if k < LANCZOS - 1:
            near = near + (halo[k, 0, v, at : at + rows] + halo[k, 1, v, at : at + rows])
        else:
            near = near + 2.0 * halo[k, sides(k, h)[0], v, at : at + rows]
        new = onsite[at : at + rows] * here - inv_wide * near
        if k:
            new = 2.0 * new - field[k - 1, v, PAD + at : PAD + at + rows]
        if k < LANCZOS - 1:
            field[k + 1, v, PAD + at : PAD + at + rows] = new
            if h == 0:
                field[k + 1, v, PAD + height :] = new[0:PAD]
            if h == PARTS - 1:
                field[k + 1, v, 0:PAD] = new[rows - PAD :]
            send(k + 1, v, h)
        note(2 * k, v, here * here)
        note(2 * k + 1, v, here * new)

    for k in range(LANCZOS):
        for v in range(vecs):
            for h in range(PARTS):
                unit(k, v, h)

    lane = lax.broadcasted_iota(jnp.int32, (vecs, 128), 1)
    line = lax.broadcasted_iota(jnp.int32, (vecs, 128), 0)
    tile = jnp.zeros((vecs, 128), jnp.float32)
    for d in range(2 * LANCZOS):
        for v in range(vecs):
            whole = jnp.sum(jnp.sum(sums[d, v], axis=0, keepdims=True), axis=1, keepdims=True)
            tile = jnp.where((lane == d) & (line == v), whole, tile)

    def exchange(leg, slots, index, size, target, tile):
        mine[leg] = tile
        slots[index] = tile

        def body(i, carry):
            pltpu.make_async_remote_copy(
                src_ref=mine.at[leg], dst_ref=slots.at[index],
                send_sem=red_send.at[leg], recv_sem=red_recv.at[leg],
                device_id=(target(i),), device_id_type=mesh_id,
            ).start()
            return carry

        lax.fori_loop(1, size, body, 0)
        rest = slots.at[pl.ds(0, size - 1)]
        pltpu.make_async_copy(rest, rest, red_recv.at[leg]).wait()

    exchange(0, near_part, member, RING, peer, tile)
    pairs = [two_sum(near_part[i], near_part[i + 1]) for i in range(0, RING, 2)]
    while len(pairs) > 1:
        pairs = [add(x, y) for x, y in zip(pairs[::2], pairs[1::2])]
    high, low = pairs[0]
    tile = jnp.where(lane < FAR, high, pltpu.roll(low, FAR, 1))
    exchange(1, far_part, ring, rings, far, tile)
    pairs = []
    for i in range(rings):
        both = far_part[i]
        pairs.append((both, pltpu.roll(both, FAR, 1)))
    while len(pairs) > 1:
        pairs = [add(x, y) for x, y in zip(pairs[::2], pairs[1::2])]
    high, low = pairs[0]

    def pick(x, d):
        return jnp.broadcast_to(x[:, d : d + 1], (vecs, 128))

    dots = [(pick(high, d), pick(low, d)) for d in range(2 * LANCZOS)]
    nu, diag, offd = coefficients(dots)
    diag = [width * a + mean for a in diag]
    offd = [width * b for b in offd]
    third, moments = chebyshev(diag, offd, nu, mean, width)

    for v in range(vecs):
        weights = [jnp.concatenate([x[v : v + 1]] * (lanes // 128), axis=1) for x in third]
        total = weights[0] * field[0, v, PAD : PAD + height]
        for k in range(1, len(weights)):
            total = total + weights[k] * field[k, v, PAD : PAD + height]
        cheb[v, 0] = total

    for ref, items in ((diag_out, diag), (offd_out, offd), (moments_out, moments)):
        at = lax.broadcasted_iota(jnp.int32, ref.shape, 1)
        value = jnp.zeros(ref.shape, jnp.float32)
        for i, item in enumerate(items):
            value = jnp.where(at == i, item[:, : ref.shape[1]], value)
        ref[...] = value

    for copy in sent:
        copy.wait_send()
    for leg, (slots, size) in enumerate(((near_part, RING), (far_part, rings))):
        rest = slots.at[pl.ds(0, size - 1)]
        pltpu.make_async_copy(rest, rest, red_send.at[leg]).wait()


def shards(count, start_vectors, levels, energies):
    vecs, _, height, lanes = start_vectors.shape
    rings = count // RING
    f32 = jnp.float32
    vmem = pl.BlockSpec(memory_space=pltpu.VMEM)
    anywhere = pl.BlockSpec(memory_space=pl.ANY)
    dma = pltpu.SemaphoreType.DMA
    return pl.pallas_call(
        functools.partial(kernel, count),
        out_shape=(
            jax.ShapeDtypeStruct(start_vectors.shape, f32),
            jax.ShapeDtypeStruct((vecs, LANCZOS), f32),
            jax.ShapeDtypeStruct((vecs, LANCZOS - 1), f32),
            jax.ShapeDtypeStruct((vecs, 6), f32),
        ),
        in_specs=[pl.BlockSpec(memory_space=pltpu.SMEM), anywhere, anywhere],
        out_specs=(vmem,) * 4,
        scratch_shapes=[
            pltpu.VMEM((LANCZOS, vecs, height + 2 * PAD, lanes), f32),
            pltpu.VMEM((LANCZOS, 2, vecs, height, lanes), f32),
            pltpu.VMEM((height, lanes), jnp.int32),
            pltpu.VMEM((height, lanes), f32),
            pltpu.VMEM((RING, vecs, 128), f32),
            pltpu.VMEM((rings, vecs, 128), f32),
            pltpu.VMEM((2, vecs, 128), f32),
            dma((vecs + 1,)),
            dma((LANCZOS, 2, vecs, PARTS)),
            dma((LANCZOS, 2, vecs, PARTS)),
            dma((2,)),
            dma((2,)),
        ],
        compiler_params=pltpu.CompilerParams(
            collective_id=0, has_side_effects=True, vmem_limit_bytes=67043328
        ),
    )(energies, start_vectors, levels)


def solution(mesh):
    in_specs = (P(None, "slab", None, None), P("slab", None, None), P())
    out_specs = (P(None, "slab", None, None), P(), P(), P())
    return jax.shard_map(
        functools.partial(shards, mesh.shape["slab"]),
        mesh=mesh, in_specs=in_specs, out_specs=out_specs, check_vma=False,
    )
```

time: 189 us -> 86.1 us (0.46)
  Pallas kernels: 183 us -> 81.5 us
    pallas_call x1, Pallas kernels: 183 us -> 81.5 us  [shards(): pl.pallas_call(functools.partial(kernel, count), out_shape=(jax.ShapeDtyp...]
where the time goes in v1:
time: 86.1 us; the launch traced here: 85.9 us
  Pallas kernels  81.5 us (95%)
  local copies, waits for them, and re-layouts  3.76 us (4%)
    pallas_call x1, Pallas kernels, shards(): pl.pallas_call(functools.partial(kernel, count), out_shape=(jax.ShapeDtyp...  81.5 us
    unnamed x10, local copies, waits for them, and re-layouts  3.76 us

profile of v1, /device:TPU:1, one launch (start us, length us, event | category | flops | bytes accessed | tf_op | source)
XLA Modules:
  0.0 85.9 jit_solution(14697685870974625760)
XLA Ops:
  0.6 81.5 %shard_map.66 = (f32[2,1,256,256]{3,2,1,0:T(8,128)}, f32[2,8]{1,0:T(2,128)}, f32[2,7]{1,0:T(2,128)}, f32[2,6]{1,0:T(2,128)}) custom-call(f32[16]{0:T(128)} %energies.1, f32[2,1,256,256]{3,2,1,0:T(8,128)} %start.1, s32[1,256,256]{2,1,0:T(8,128)} %levels.1), custom_call_target="tpu_custom_call" | custom-call | tf_op jit(solution)/shard_map/pallas_call | solution.py:341
  82.1 0.0 copy-start.2
  82.1 1.9 %copy.11 = f32[2,1,256,256]{3,2,1,0:T(8,128)} copy(f32[2,1,256,256]{3,2,1,0:T(8,128)} %get-tuple-element.8) | data formatting | bytes 1048576
  84.0 0.0 copy-done.2
  84.0 0.0 copy-start.1
  84.0 0.6 copy.12
  84.5 0.1 copy-done.1
  84.6 0.0 copy-start
  84.6 0.6 copy.13
  85.2 0.1 copy-done
  85.3 0.6 copy.14
Async XLA Ops:
  82.1 1.9 %copy-start.2 = (f32[2,8]{1,0:T(2,128)S(1)}, f32[2,8]{1,0:T(2,128)}, u32[]{:S(2)}) copy-start(f32[2,8]{1,0:T(2,128)} %get-tuple-element.9) | copy-start | bytes 196
  84.0 0.7 copy-start.1
  84.6 0.7 copy-start

commit v2 on v1

--- a/solution.py
+++ b/solution.py
@@ -9,9 +9,11 @@
 
 LANCZOS = 8
 RING = 16
-PARTS = 2
+PARTS = 4
 PAD = 8
 FAR = 64
+RETURNED = 4
+GAP = 6
 
 
 def two_sum(a, b):
@@ -125,9 +127,9 @@
 
 
 def kernel(
-    count, energies, start, levels, cheb, diag_out, offd_out, moments_out,
-    field, halo, level, onsite, near_part, far_part, mine,
-    load_sem, send_sem, recv_sem, red_send, red_recv,
+    count, energies, start, levels, terms, sums_out, table,
+    field, halo, level, onsite, near_part, mine,
+    load_sem, send_sem, recv_sem, last_sem, red_send, red_recv, known,
 ):
     me = lax.axis_index("slab")
     member = lax.rem(me, RING)
@@ -137,9 +139,18 @@
     vecs, _, height, lanes = start.shape
     rows = height // PARTS
     mesh_id = pl.DeviceIdType.MESH
-    ahead = lax.rem(me + 1, count)
-    behind = lax.rem(me + count - 1, count)
-
+
+    def away(distance):
+        return lax.rem(me + distance, count), lax.rem(me + count - distance, count)
+
+    ahead, behind = away(1)
+
+    def signal(sem, to):
+        pl.semaphore_signal(sem, inc=1, device_id=(to,), device_id_type=mesh_id)
+
+    barrier = pltpu.get_barrier_semaphore()
+    for to in (ahead, behind):
+        signal(barrier, to)
     loads = [
         pltpu.make_async_copy(start.at[v, 0], field.at[0, v, pl.ds(PAD, height)], load_sem.at[v]) for v in range(vecs)
     ]
@@ -153,31 +164,50 @@
     def far(i):
         return lax.rem(me + i * RING, count)
 
-    barrier = pltpu.get_barrier_semaphore()
-
-    def greet(to):
-        pl.semaphore_signal(barrier, inc=1, device_id=(to,), device_id_type=mesh_id)
-
-    def greet_peer(i, carry):
-        greet(peer(i))
-        return carry
-
-    def greet_far(i, carry):
-        greet(far(i))
-        return carry
-
-    greet(ahead)
-    greet(behind)
-    lax.fori_loop(1, RING, greet_peer, 0)
-    lax.fori_loop(1, rings, greet_far, 0)
+    rounds = (count // 2).bit_length() - 1
+
+    def spread(i):
+        if i:
+            pl.semaphore_wait(known.at[i - 1], 2)
+        if i < rounds:
+            for to in away(2**i):
+                signal(known.at[i], to)
+
+    def part_copy(k, v, h, side):
+        to = ahead if side == 0 else behind
+        at = h * rows
+        sender = last_sem.at[side] if k == LANCZOS - 1 else send_sem.at[side]
+        return pltpu.make_async_remote_copy(
+            src_ref=field.at[k, v, pl.ds(PAD + at, rows)],
+            dst_ref=halo.at[k, side, v, pl.ds(at, rows)],
+            send_sem=sender, recv_sem=recv_sem.at[k % 2, side, v, h],
+            device_id=(to,), device_id_type=mesh_id,
+        )
+
+    def sides(k, h):
+        if k < LANCZOS - 1:
+            return (0, 1)
+        return (0,) if h < PARTS // 2 else (1,)
+
+    def send(k, v, h):
+        for side in sides(k, h):
+            part_copy(k, v, h, side).start()
+
+    pl.semaphore_wait(barrier, 2)
+    for v in range(vecs):
+        loads[v].wait()
+        for h in range(PARTS):
+            send(0, v, h)
 
     values = [energies[i] for i in range(energies.shape[0])]
     mean = sum(values[1:], values[0]) * (1.0 / len(values))
-    spread = [(x - mean) * (x - mean) for x in values]
-    spread = sum(spread[1:], spread[0]) * (1.0 / len(values))
-    width = 2.0 * jnp.sqrt(jnp.full((1, 128), spread + 6.0, jnp.float32))
+    spread_of = [(x - mean) * (x - mean) for x in values]
+    spread_of = sum(spread_of[1:], spread_of[0]) * (1.0 / len(values))
+    width = 2.0 * jnp.sqrt(jnp.full((1, 128), spread_of + 6.0, jnp.float32))
     inv_width = 1.0 / width
     inv_wide = jnp.concatenate([inv_width] * (lanes // 128), axis=1)
+    table[0:1] = width
+    table[1:2] = jnp.full((1, 128), mean, jnp.float32)
 
     loads[vecs].wait()
     for at in range(0, height, 64):
@@ -186,38 +216,10 @@
         for i in range(1, len(values)):
             energy = jnp.where(ids == i, values[i] - mean, energy)
         onsite[at : at + 64] = energy * inv_wide
-
-    pl.semaphore_wait(barrier, 2 + RING - 1 + rings - 1)
-
-    def part_copy(k, v, h, side):
-        to = ahead if side == 0 else behind
-        at = h * rows
-        return pltpu.make_async_remote_copy(
-            src_ref=field.at[k, v, pl.ds(PAD + at, rows)],
-            dst_ref=halo.at[k, side, v, pl.ds(at, rows)],
-            send_sem=send_sem.at[k, side, v, h], recv_sem=recv_sem.at[k, side, v, h],
-            device_id=(to,), device_id_type=mesh_id,
-        )
-
-    def sides(k, h):
-        if k < LANCZOS - 1:
-            return (0, 1)
-        return (0,) if h < PARTS // 2 else (1,)
-
-    sent = []
-
-    def send(k, v, h):
-        for side in sides(k, h):
-            copy = part_copy(k, v, h, side)
-            copy.start()
-            sent.append(copy)
-
     for v in range(vecs):
-        loads[v].wait()
-        for h in range(PARTS):
-            send(0, v, h)
         field[0, v, 0:PAD] = field[0, v, height : height + PAD]
         field[0, v, PAD + height :] = field[0, v, PAD : 2 * PAD]
+        terms[0, v] = field[0, v, PAD : PAD + height]
 
     def tile_sum(x):
         total = x[0:8]
@@ -254,13 +256,21 @@
             if h == PARTS - 1:
                 field[k + 1, v, 0:PAD] = new[rows - PAD :]
             send(k + 1, v, h)
+        if k + 1 < RETURNED:
+            terms[k + 1, v, at : at + rows] = new
         note(2 * k, v, here * here)
         note(2 * k + 1, v, here * new)
 
-    for k in range(LANCZOS):
-        for v in range(vecs):
-            for h in range(PARTS):
-                unit(k, v, h)
+    units = [(k, v, h) for k in range(LANCZOS) for v in range(vecs) for h in range(PARTS)]
+    turn = 0
+    for i, (k, v, h) in enumerate(units):
+        if i == turn * GAP and turn <= rounds:
+            spread(turn)
+            turn += 1
+        unit(k, v, h)
+    while turn <= rounds:
+        spread(turn)
+        turn += 1
 
     lane = lax.broadcasted_iota(jnp.int32, (vecs, 128), 1)
     line = lax.broadcasted_iota(jnp.int32, (vecs, 128), 0)
@@ -292,10 +302,24 @@
         pairs = [add(x, y) for x, y in zip(pairs[::2], pairs[1::2])]
     high, low = pairs[0]
     tile = jnp.where(lane < FAR, high, pltpu.roll(low, FAR, 1))
-    exchange(1, far_part, ring, rings, far, tile)
+    exchange(1, sums_out, ring, rings, far, tile)
+
+    for side in range(2):
+        whole = halo.at[pl.ds(0, LANCZOS - 1), 0]
+        pltpu.make_async_copy(whole, whole, send_sem.at[side]).wait()
+        half = halo.at[0, 0, pl.ds(0, vecs), pl.ds(0, height // 2)]
+        pltpu.make_async_copy(half, half, last_sem.at[side]).wait()
+    for leg, (slots, size) in enumerate(((near_part, RING), (sums_out, rings))):
+        rest = slots.at[pl.ds(0, size - 1)]
+        pltpu.make_async_copy(rest, rest, red_send.at[leg]).wait()
+
+
+def finish(terms, parts, table, cheb, diag_out, offd_out, moments_out, result, out_sem):
+    _, vecs, height, lanes = terms.shape
+    width, mean = table[0:1], table[1:2]
     pairs = []
-    for i in range(rings):
-        both = far_part[i]
+    for i in range(parts.shape[0]):
+        both = parts[i]
         pairs.append((both, pltpu.roll(both, FAR, 1)))
     while len(pairs) > 1:
         pairs = [add(x, y) for x, y in zip(pairs[::2], pairs[1::2])]
@@ -310,12 +334,15 @@
     offd = [width * b for b in offd]
     third, moments = chebyshev(diag, offd, nu, mean, width)
 
+    copies = []
     for v in range(vecs):
         weights = [jnp.concatenate([x[v : v + 1]] * (lanes // 128), axis=1) for x in third]
-        total = weights[0] * field[0, v, PAD : PAD + height]
+        total = weights[0] * terms[0, v]
         for k in range(1, len(weights)):
-            total = total + weights[k] * field[k, v, PAD : PAD + height]
-        cheb[v, 0] = total
+            total = total + weights[k] * terms[k, v]
+        result[v] = total
+        copies.append(pltpu.make_async_copy(result.at[v], cheb.at[v, 0], out_sem.at[v]))
+        copies[-1].start()
 
     for ref, items in ((diag_out, diag), (offd_out, offd), (moments_out, moments)):
         at = lax.broadcasted_iota(jnp.int32, ref.shape, 1)
@@ -323,12 +350,8 @@
         for i, item in enumerate(items):
             value = jnp.where(at == i, item[:, : ref.shape[1]], value)
         ref[...] = value
-
-    for copy in sent:
-        copy.wait_send()
-    for leg, (slots, size) in enumerate(((near_part, RING), (far_part, rings))):
-        rest = slots.at[pl.ds(0, size - 1)]
-        pltpu.make_async_copy(rest, rest, red_send.at[leg]).wait()
+    for copy in copies:
+        copy.wait()
 
 
 def shards(count, start_vectors, levels, energies):
@@ -338,34 +361,47 @@
     vmem = pl.BlockSpec(memory_space=pltpu.VMEM)
     anywhere = pl.BlockSpec(memory_space=pl.ANY)
     dma = pltpu.SemaphoreType.DMA
+    terms, parts, table = pl.pallas_call(
+        functools.partial(kernel, count),
+        out_shape=(
+            pltpu.VMEM((RETURNED, vecs, height, lanes), f32),
+            pltpu.VMEM((rings, vecs, 128), f32),
+            pltpu.VMEM((2, 128), f32),
+        ),
+        in_specs=[pl.BlockSpec(memory_space=pltpu.SMEM), anywhere, anywhere],
+        out_specs=(vmem,) * 3,
+        scratch_shapes=[
+            pltpu.VMEM((LANCZOS, vecs, height + 2 * PAD, lanes), f32),
+            pltpu.VMEM((LANCZOS, 2, vecs, height, lanes), f32),
+            pltpu.VMEM((height, lanes), jnp.int32),
+            pltpu.VMEM((height, lanes), f32),
+            pltpu.VMEM((RING, vecs, 128), f32),
+            pltpu.VMEM((2, vecs, 128), f32),
+            dma((vecs + 1,)),
+            dma((2,)),
+            dma((2, 2, vecs, PARTS)),
+            dma((2,)),
+            dma((2,)),
+            dma((2,)),
+            pltpu.SemaphoreType.REGULAR(((count // 2).bit_length() - 1,)),
+        ],
+        compiler_params=pltpu.CompilerParams(
+            collective_id=0, has_side_effects=True, vmem_limit_bytes=60 << 20
+        ),
+    )(energies, start_vectors, levels)
     return pl.pallas_call(
-        functools.partial(kernel, count),
+        finish,
         out_shape=(
             jax.ShapeDtypeStruct(start_vectors.shape, f32),
             jax.ShapeDtypeStruct((vecs, LANCZOS), f32),
             jax.ShapeDtypeStruct((vecs, LANCZOS - 1), f32),
             jax.ShapeDtypeStruct((vecs, 6), f32),
         ),
-        in_specs=[pl.BlockSpec(memory_space=pltpu.SMEM), anywhere, anywhere],
-        out_specs=(vmem,) * 4,
-        scratch_shapes=[
-            pltpu.VMEM((LANCZOS, vecs, height + 2 * PAD, lanes), f32),
-            pltpu.VMEM((LANCZOS, 2, vecs, height, lanes), f32),
-            pltpu.VMEM((height, lanes), jnp.int32),
-            pltpu.VMEM((height, lanes), f32),
-            pltpu.VMEM((RING, vecs, 128), f32),
-            pltpu.VMEM((rings, vecs, 128), f32),
-            pltpu.VMEM((2, vecs, 128), f32),
-            dma((vecs + 1,)),
-            dma((LANCZOS, 2, vecs, PARTS)),
-            dma((LANCZOS, 2, vecs, PARTS)),
-            dma((2,)),
-            dma((2,)),
-        ],
-        compiler_params=pltpu.CompilerParams(
-            collective_id=0, has_side_effects=True, vmem_limit_bytes=67043328
-        ),
-    )(energies, start_vectors, levels)
+        in_specs=[vmem] * 3,
+        out_specs=(anywhere, vmem, vmem, vmem),
+        scratch_shapes=[pltpu.VMEM((vecs, height, lanes), f32), dma((vecs,))],
+        compiler_params=pltpu.CompilerParams(vmem_limit_bytes=16 << 20),
+    )(terms, parts, table)
 
 
 def solution(mesh):

time: 86.1 us -> 76.1 us (0.88)
  Pallas kernels: 81.5 us -> 75.3 us
  local copies, waits for them, and re-layouts: 3.76 us -> 0 us
    pallas_call x1 -> x2, Pallas kernels: 81.5 us -> 75.3 us  [the longest x1 72.8 us: shards(): pl.pallas_call(functools.partial(kernel, count), out_shape=(pltpu.VMEM((R...]
    unnamed x10 -> x0, local copies, waits for them, and re-layouts: 3.76 us -> none
where the time goes in v2:
time: 76.1 us; the launch traced here: 75.9 us
  Pallas kernels  75.3 us (99%)
    pallas_call x1, Pallas kernels, shards(): pl.pallas_call(functools.partial(kernel, count), out_shape=(pltpu.VMEM((R...  72.8 us
    pallas_call x1, Pallas kernels, shards(): pl.pallas_call(finish, out_shape=(jax.ShapeDtypeStruct(start_vectors.shap...  2.51 us

profile of v2, /device:TPU:1, one launch (start us, length us, event | category | flops | bytes accessed | tf_op | source)
XLA Modules:
  0.0 75.9 jit_solution(2009871776083786691)
XLA Ops:
  0.6 72.8 %shard_map.66 = (f32[4,2,256,256]{3,2,1,0:T(8,128)S(1)}, f32[32,2,128]{2,1,0:T(2,128)S(1)}, f32[2,128]{1,0:T(2,128)S(1)}) custom-call(f32[16]{0:T(128)} %energies.1, f32[2,1,256,256]{3,2,1,0:T(8,128)} %start.1, s32[1,256,256]{2,1,0:T(8,128)} %levels.1), custom_call_target="tpu_custom_call" | custom-call | tf_op jit(solution)/shard_map/pallas_call | solution.py:364
  73.4 2.5 %shard_map.67 = (f32[2,1,256,256]{3,2,1,0:T(8,128)}, f32[2,8]{1,0:T(2,128)}, f32[2,7]{1,0:T(2,128)}, f32[2,6]{1,0:T(2,128)}) custom-call(f32[4,2,256,256]{3,2,1,0:T(8,128)S(1)} %get-tuple-element.7.terms, f32[32,2,128]{2,1,0:T(2,128)S(1)} %get-tuple-element.8.parts, f32[2,128]{1,0:T(2,128)S(1)} %get-tuple-element.9.table), custom_call_target="tpu_custom_call" | custom-call | tf_op jit(solution)/shard_map/pallas_call | solution.py:392

commit v3 on v2

--- a/solution.py
+++ b/solution.py
@@ -9,11 +9,11 @@
 
 LANCZOS = 8
 RING = 16
-PARTS = 4
+PARTS = 8
 PAD = 8
 FAR = 64
 RETURNED = 4
-GAP = 6
+GAP = 12
 
 
 def two_sum(a, b):
@@ -27,66 +27,63 @@
     return s, b - (s - a)
 
 
-def split(a):
-    t = 4097.0 * a
-    high = t - (t - a)
-    return high, a - high
-
-
-def two_prod(a, b):
-    p = a * b
-    ah, al = split(a)
-    bh, bl = split(b)
-    return p, ((ah * bh - p) + ah * bl + al * bh) + al * bl
-
-
 def add(x, y):
     s, e = two_sum(x[0], y[0])
     return quick(s, e + (x[1] + y[1]))
 
 
-def sub(x, y):
-    return add(x, (-y[0], -y[1]))
-
-
-def mul(x, y):
-    p, e = two_prod(x[0], y[0])
-    return quick(p, e + (x[0] * y[1] + x[1] * y[0]))
-
-
-def scale(x, c):
-    return x[0] * c, x[1] * c
-
-
-def div(x, y):
-    q = x[0] / y[0]
-    p, e = two_prod(q, y[0])
-    return quick(q, (((x[0] - p) - e) + (x[1] - q * y[1])) / y[0])
+def wide(x):
+    t = 4097.0 * x[0]
+    upper = t - (t - x[0])
+    return x[0], x[1], upper, x[0] - upper
+
+
+def times(x, y):
+    p = x[0] * y[0]
+    e = ((x[2] * y[2] - p) + x[2] * y[3] + x[3] * y[2]) + x[3] * y[3]
+    return p, e + (x[0] * y[1] + x[1] * y[0])
+
+
+def minus(x, y):
+    s, e = two_sum(x[0], -y[0])
+    return s, e + (x[1] - y[1])
+
+
+def twice(x):
+    return tuple(2.0 * part for part in x)
+
+
+def inverse(x):
+    q = 1.0 / x[0]
+    p, e = times(wide((q, 0.0 * q)), x)
+    return wide(quick(q, q * ((1.0 - p) - e)))
 
 
 def coefficients(dots):
     count = len(dots)
-    norm = dots[0]
-    nu = [(norm[0] / norm[0], norm[0] * 0.0), div(dots[1], norm)]
+    norm = inverse(wide(dots[0]))
+    nu = [wide((norm[0] * 0.0 + 1.0, norm[0] * 0.0)), wide(quick(*times(wide(dots[1]), norm)))]
     for k in range(2, count):
-        nu.append(sub(scale(div(dots[k], norm), 2.0), nu[k % 2]))
-    row, before = nu, None
-    diag, square = [], []
+        nu.append(wide(quick(*minus(twice(times(wide(dots[k]), norm)), nu[k % 2]))))
+    row, before, square = nu, None, None
+    diag, offd = [], []
     for k in range(LANCZOS):
-        if k == 0:
-            alpha = row[1]
-        else:
-            alpha = div(sub(scale(row[k + 1], 0.5), mul(square[-1], before[k])), row[k])
-        diag.append(alpha)
+        inv = nu[0] if k == 0 else inverse(row[k])
+        top = twice(row[1])[:2] if k == 0 else minus(row[k + 1], times(square, before[k]))
+        alpha = wide(quick(*times(wide(quick(*top)), inv)))
+        diag.append(0.5 * alpha[0])
         if k == LANCZOS - 1:
             break
         new = [None] * count
         for l in range(k + 1, count - 1 - k):
-            x = sub(scale(add(row[l + 1], row[l - 1]), 0.5), mul(alpha, row[l]))
-            new[l] = sub(x, mul(square[-1], before[l])) if k else x
-        square.append(div(new[k + 1], row[k] if k == 0 else scale(row[k], 2.0)))
+            s, e = two_sum(row[l + 1][0], row[l - 1][0])
+            x = minus((s, e + (row[l + 1][1] + row[l - 1][1])), times(alpha, row[l]))
+            new[l] = wide(quick(*(minus(x, times(square, before[l])) if k else x)))
+        square = times(twice(new[1]) if k == 0 else new[k + 1], inv)
+        square = wide(quick(*square))
+        offd.append(0.5 * jnp.sqrt(square[0]))
         before, row = row, new
-    return [x[0] for x in nu], [x[0] for x in diag], [jnp.sqrt(x[0]) for x in square]
+    return [x[0] for x in nu], diag, offd
 
 
 def chebyshev(diag, offd, nu, centre, width):
@@ -128,7 +125,23 @@
 
 def kernel(
     count, energies, start, levels, terms, sums_out, table,
-    field, halo, level, onsite, near_part, mine,
+    field, halo, level, onsite, near_part, mine, scalars,
+):
+    vecs, rounds = start.shape[0], (count // 2).bit_length() - 1
+    dma = pltpu.SemaphoreType.DMA
+    body = functools.partial(
+        steps, count, energies, start, levels, terms, sums_out, table,
+        field, halo, level, onsite, near_part, mine, scalars,
+    )
+    pl.run_scoped(
+        body, dma((vecs + 2,)), dma((2,)), dma((2, 2, vecs, PARTS)), dma((2,)), dma((2,)), dma((2,)),
+        pltpu.SemaphoreType.REGULAR((rounds,)),
+    )
+
+
+def steps(
+    count, energies, start, levels, terms, sums_out, table,
+    field, halo, level, onsite, near_part, mine, scalars,
     load_sem, send_sem, recv_sem, last_sem, red_send, red_recv, known,
 ):
     me = lax.axis_index("slab")
@@ -155,6 +168,7 @@
         pltpu.make_async_copy(start.at[v, 0], field.at[0, v, pl.ds(PAD, height)], load_sem.at[v]) for v in range(vecs)
     ]
     loads.append(pltpu.make_async_copy(levels.at[0], level, load_sem.at[vecs]))
+    loads.append(pltpu.make_async_copy(energies, scalars, load_sem.at[vecs + 1]))
     for copy in loads:
         copy.start()
 
@@ -199,7 +213,8 @@
         for h in range(PARTS):
             send(0, v, h)
 
-    values = [energies[i] for i in range(energies.shape[0])]
+    loads[vecs + 1].wait()
+    values = [scalars[i] for i in range(energies.shape[0])]
     mean = sum(values[1:], values[0]) * (1.0 / len(values))
     spread_of = [(x - mean) * (x - mean) for x in values]
     spread_of = sum(spread_of[1:], spread_of[0]) * (1.0 / len(values))
@@ -261,60 +276,68 @@
         note(2 * k, v, here * here)
         note(2 * k + 1, v, here * new)
 
+    lane = lax.broadcasted_iota(jnp.int32, (vecs, 128), 1)
+    line = lax.broadcasted_iota(jnp.int32, (vecs, 128), 0)
+
+    def gather(tile, k, v):
+        for d in (2 * k, 2 * k + 1):
+            whole = jnp.sum(jnp.sum(sums[d, v], axis=0, keepdims=True), axis=1, keepdims=True)
+            tile = jnp.where((lane == d) & (line == v), whole, tile)
+        return tile
+
     units = [(k, v, h) for k in range(LANCZOS) for v in range(vecs) for h in range(PARTS)]
+    tile = jnp.zeros((vecs, 128), jnp.float32)
     turn = 0
     for i, (k, v, h) in enumerate(units):
         if i == turn * GAP and turn <= rounds:
             spread(turn)
             turn += 1
         unit(k, v, h)
+        if h == PARTS - 1:
+            tile = gather(tile, k, v)
     while turn <= rounds:
         spread(turn)
         turn += 1
 
-    lane = lax.broadcasted_iota(jnp.int32, (vecs, 128), 1)
-    line = lax.broadcasted_iota(jnp.int32, (vecs, 128), 0)
-    tile = jnp.zeros((vecs, 128), jnp.float32)
-    for d in range(2 * LANCZOS):
-        for v in range(vecs):
-            whole = jnp.sum(jnp.sum(sums[d, v], axis=0, keepdims=True), axis=1, keepdims=True)
-            tile = jnp.where((lane == d) & (line == v), whole, tile)
-
     def exchange(leg, slots, index, size, target, tile):
         mine[leg] = tile
         slots[index] = tile
 
-        def body(i, carry):
+        for i in sorted(range(1, size), key=lambda i: abs(2 * i - size)):
             pltpu.make_async_remote_copy(
                 src_ref=mine.at[leg], dst_ref=slots.at[index],
                 send_sem=red_send.at[leg], recv_sem=red_recv.at[leg],
                 device_id=(target(i),), device_id_type=mesh_id,
             ).start()
-            return carry
-
-        lax.fori_loop(1, size, body, 0)
+
+    def arrived(leg, slots, size):
         rest = slots.at[pl.ds(0, size - 1)]
         pltpu.make_async_copy(rest, rest, red_recv.at[leg]).wait()
 
+    def sent(leg, slots, size):
+        rest = slots.at[pl.ds(0, size - 1)]
+        pltpu.make_async_copy(rest, rest, red_send.at[leg]).wait()
+
     exchange(0, near_part, member, RING, peer, tile)
+    for side in range(2):
+        whole = halo.at[pl.ds(0, LANCZOS - 1), 0]
+        pltpu.make_async_copy(whole, whole, send_sem.at[side]).wait()
+        half = halo.at[0, 0, pl.ds(0, vecs), pl.ds(0, height // 2)]
+        pltpu.make_async_copy(half, half, last_sem.at[side]).wait()
+    arrived(0, near_part, RING)
     pairs = [two_sum(near_part[i], near_part[i + 1]) for i in range(0, RING, 2)]
     while len(pairs) > 1:
         pairs = [add(x, y) for x, y in zip(pairs[::2], pairs[1::2])]
     high, low = pairs[0]
     tile = jnp.where(lane < FAR, high, pltpu.roll(low, FAR, 1))
     exchange(1, sums_out, ring, rings, far, tile)
-
-    for side in range(2):
-        whole = halo.at[pl.ds(0, LANCZOS - 1), 0]
-        pltpu.make_async_copy(whole, whole, send_sem.at[side]).wait()
-        half = halo.at[0, 0, pl.ds(0, vecs), pl.ds(0, height // 2)]
-        pltpu.make_async_copy(half, half, last_sem.at[side]).wait()
-    for leg, (slots, size) in enumerate(((near_part, RING), (sums_out, rings))):
-        rest = slots.at[pl.ds(0, size - 1)]
-        pltpu.make_async_copy(rest, rest, red_send.at[leg]).wait()
-
-
-def finish(terms, parts, table, cheb, diag_out, offd_out, moments_out, result, out_sem):
+    sent(0, near_part, RING)
+    arrived(1, sums_out, rings)
+
+    sent(1, sums_out, rings)
+
+
+def finish(terms, parts, table, cheb, diag_out, offd_out, moments_out, result, diag_own, offd_own, moments_own, out_sem):
     _, vecs, height, lanes = terms.shape
     width, mean = table[0:1], table[1:2]
     pairs = []
@@ -335,21 +358,25 @@
     third, moments = chebyshev(diag, offd, nu, mean, width)
 
     copies = []
+
+    def put(source, target):
+        copies.append(pltpu.make_async_copy(source, target, out_sem.at[len(copies)]))
+        copies[-1].start()
+
     for v in range(vecs):
         weights = [jnp.concatenate([x[v : v + 1]] * (lanes // 128), axis=1) for x in third]
         total = weights[0] * terms[0, v]
         for k in range(1, len(weights)):
             total = total + weights[k] * terms[k, v]
         result[v] = total
-        copies.append(pltpu.make_async_copy(result.at[v], cheb.at[v, 0], out_sem.at[v]))
-        copies[-1].start()
-
-    for ref, items in ((diag_out, diag), (offd_out, offd), (moments_out, moments)):
-        at = lax.broadcasted_iota(jnp.int32, ref.shape, 1)
-        value = jnp.zeros(ref.shape, jnp.float32)
+        put(result.at[v], cheb.at[v, 0])
+    for own, ref, items in ((diag_own, diag_out, diag), (offd_own, offd_out, offd), (moments_own, moments_out, moments)):
+        at = lax.broadcasted_iota(jnp.int32, own.shape, 1)
+        value = jnp.zeros(own.shape, jnp.float32)
         for i, item in enumerate(items):
-            value = jnp.where(at == i, item[:, : ref.shape[1]], value)
-        ref[...] = value
+            value = jnp.where(at == i, item[:, : own.shape[1]], value)
+        own[...] = value
+        put(own, ref)
     for copy in copies:
         copy.wait()
 
@@ -368,7 +395,7 @@
             pltpu.VMEM((rings, vecs, 128), f32),
             pltpu.VMEM((2, 128), f32),
         ),
-        in_specs=[pl.BlockSpec(memory_space=pltpu.SMEM), anywhere, anywhere],
+        in_specs=[anywhere] * 3,
         out_specs=(vmem,) * 3,
         scratch_shapes=[
             pltpu.VMEM((LANCZOS, vecs, height + 2 * PAD, lanes), f32),
@@ -377,13 +404,7 @@
             pltpu.VMEM((height, lanes), f32),
             pltpu.VMEM((RING, vecs, 128), f32),
             pltpu.VMEM((2, vecs, 128), f32),
-            dma((vecs + 1,)),
-            dma((2,)),
-            dma((2, 2, vecs, PARTS)),
-            dma((2,)),
-            dma((2,)),
-            dma((2,)),
-            pltpu.SemaphoreType.REGULAR(((count // 2).bit_length() - 1,)),
+            pltpu.SMEM(energies.shape, f32),
         ],
         compiler_params=pltpu.CompilerParams(
             collective_id=0, has_side_effects=True, vmem_limit_bytes=60 << 20
@@ -398,8 +419,14 @@
             jax.ShapeDtypeStruct((vecs, 6), f32),
         ),
         in_specs=[vmem] * 3,
-        out_specs=(anywhere, vmem, vmem, vmem),
-        scratch_shapes=[pltpu.VMEM((vecs, height, lanes), f32), dma((vecs,))],
+        out_specs=(anywhere,) * 4,
+        scratch_shapes=[
+            pltpu.VMEM((vecs, height, lanes), f32),
+            pltpu.VMEM((vecs, LANCZOS), f32),
+            pltpu.VMEM((vecs, LANCZOS - 1), f32),
+            pltpu.VMEM((vecs, 6), f32),
+            dma((vecs + 3,)),
+        ],
         compiler_params=pltpu.CompilerParams(vmem_limit_bytes=16 << 20),
     )(terms, parts, table)
 

time: 76.1 us -> 73.5 us (0.966)
  Pallas kernels: 75.3 us -> 72.8 us
    pallas_call x1, Pallas kernels: 72.8 us -> 70.9 us  [shards(): pl.pallas_call(functools.partial(kernel, count), out_shape=(pltpu.VMEM((R...]
where the time goes in v3:
time: 73.5 us; the launch traced here: 73.4 us
  Pallas kernels  72.8 us (99%)
    pallas_call x1, Pallas kernels, shards(): pl.pallas_call(functools.partial(kernel, count), out_shape=(pltpu.VMEM((R...  70.9 us
    pallas_call x1, Pallas kernels, shards(): pl.pallas_call(finish, out_shape=(jax.ShapeDtypeStruct(start_vectors.shap...  1.84 us

profile of v3, /device:TPU:1, one launch (start us, length us, event | category | flops | bytes accessed | tf_op | source)
XLA Modules:
  0.0 73.4 jit_solution(7660376061261793182)
XLA Ops:
  0.6 70.9 %shard_map.66 = (f32[4,2,256,256]{3,2,1,0:T(8,128)S(1)}, f32[32,2,128]{2,1,0:T(2,128)S(1)}, f32[2,128]{1,0:T(2,128)S(1)}) custom-call(f32[16]{0:T(128)} %energies.1, f32[2,1,256,256]{3,2,1,0:T(8,128)} %start.1, s32[1,256,256]{2,1,0:T(8,128)} %levels.1), custom_call_target="tpu_custom_call" | custom-call | tf_op jit(solution)/shard_map/pallas_call | solution.py:391
  71.6 1.8 %shard_map.67 = (f32[2,1,256,256]{3,2,1,0:T(8,128)}, f32[2,8]{1,0:T(2,128)}, f32[2,7]{1,0:T(2,128)}, f32[2,6]{1,0:T(2,128)}) custom-call(f32[4,2,256,256]{3,2,1,0:T(8,128)S(1)} %get-tuple-element.7.terms, f32[32,2,128]{2,1,0:T(2,128)S(1)} %get-tuple-element.8.parts, f32[2,128]{1,0:T(2,128)S(1)} %get-tuple-element.9.table), custom_call_target="tpu_custom_call" | custom-call | tf_op jit(solution)/shard_map/pallas_call | solution.py:413

commit v4 on v3

--- a/solution.py
+++ b/solution.py
@@ -13,6 +13,7 @@
 PAD = 8
 FAR = 64
 RETURNED = 4
+DIRECT = 13
 GAP = 12
 
 
@@ -134,7 +135,8 @@
         field, halo, level, onsite, near_part, mine, scalars,
     )
     pl.run_scoped(
-        body, dma((vecs + 2,)), dma((2,)), dma((2, 2, vecs, PARTS)), dma((2,)), dma((2,)), dma((2,)),
+        body, dma((vecs + 2,)), dma((2,)), dma((3, 2, vecs, PARTS)), dma((2,)), dma((2,)), dma((2,)), dma((vecs,)),
+        pltpu.SemaphoreType.REGULAR(()),
         pltpu.SemaphoreType.REGULAR((rounds,)),
     )
 
@@ -142,7 +144,7 @@
 def steps(
     count, energies, start, levels, terms, sums_out, table,
     field, halo, level, onsite, near_part, mine, scalars,
-    load_sem, send_sem, recv_sem, last_sem, red_send, red_recv, known,
+    load_sem, send_sem, recv_sem, last_sem, red_send, red_recv, relay_sem, near_sem, known,
 ):
     me = lax.axis_index("slab")
     member = lax.rem(me, RING)
@@ -161,9 +163,29 @@
     def signal(sem, to):
         pl.semaphore_signal(sem, inc=1, device_id=(to,), device_id_type=mesh_id)
 
+    relay = RING - 2
+    is_first, is_last = (count - me) // count, (me + 1) // count
+
+    def is_device(i):
+        return (count - lax.rem(me + count - i, count)) // count
+
+    is_relay = is_device(relay)
+    before_relay, after_relay = is_device(relay - 1), is_device(relay + 1)
+
     barrier = pltpu.get_barrier_semaphore()
-    for to in (ahead, behind):
-        signal(barrier, to)
+
+    @pl.when(before_relay == 0)
+    def _():
+        signal(barrier, ahead + is_last * (relay - ahead))
+
+    @pl.when(after_relay == 0)
+    def _():
+        signal(barrier, behind)
+
+    @pl.when(is_relay == 1)
+    def _():
+        signal(barrier, 0)
+
     loads = [
         pltpu.make_async_copy(start.at[v, 0], field.at[0, v, pl.ds(PAD, height)], load_sem.at[v]) for v in range(vecs)
     ]
@@ -187,14 +209,18 @@
             for to in away(2**i):
                 signal(known.at[i], to)
 
-    def part_copy(k, v, h, side):
+    def part_copy(k, v, h, side, leaving=False):
         to = ahead if side == 0 else behind
+        slot, sem = k, k % 2
+        if leaving and k == 0 and side == 1 and v * PARTS + h < DIRECT:
+            to = to + is_first * (relay - to)
+            slot, sem = is_first * LANCZOS, is_first * 2
         at = h * rows
         sender = last_sem.at[side] if k == LANCZOS - 1 else send_sem.at[side]
         return pltpu.make_async_remote_copy(
             src_ref=field.at[k, v, pl.ds(PAD + at, rows)],
-            dst_ref=halo.at[k, side, v, pl.ds(at, rows)],
-            send_sem=sender, recv_sem=recv_sem.at[k % 2, side, v, h],
+            dst_ref=halo.at[slot, side, v, pl.ds(at, rows)],
+            send_sem=sender, recv_sem=recv_sem.at[sem, side, v, h],
             device_id=(to,), device_id_type=mesh_id,
         )
 
@@ -205,13 +231,44 @@
 
     def send(k, v, h):
         for side in sides(k, h):
-            part_copy(k, v, h, side).start()
-
-    pl.semaphore_wait(barrier, 2)
+            if k == 0 and side == 1 and v * PARTS + h >= DIRECT:
+                pl.when(is_first == 0)(part_copy(k, v, h, side).start)
+            else:
+                part_copy(k, v, h, side, True).start()
+
+    def send_rest():
+        for i in range(DIRECT, vecs * PARTS):
+            pl.when(is_first == 1)(part_copy(0, i // PARTS, i % PARTS, 1).start)
+
+    @pl.when(is_relay == 0)
+    def _():
+        pl.semaphore_wait(barrier, 2)
+
+    @pl.when(is_relay == 1)
+    def _():
+        pl.semaphore_wait(near_sem, 2)
+
+    @pl.when(before_relay + after_relay == 1)
+    def _():
+        signal(near_sem, relay)
+
     for v in range(vecs):
         loads[v].wait()
         for h in range(PARTS):
             send(0, v, h)
+
+    def forward(v, h):
+        @pl.when(is_relay == 1)
+        def _():
+            if v + h == 0:
+                pl.semaphore_wait(barrier, 1)
+            part = halo.at[LANCZOS, 1, v, pl.ds(h * rows, rows)]
+            pltpu.make_async_copy(part, part, recv_sem.at[2, 1, v, h]).wait()
+            pltpu.make_async_remote_copy(
+                src_ref=part, dst_ref=halo.at[0, 1, v, pl.ds(h * rows, rows)],
+                send_sem=relay_sem.at[v], recv_sem=recv_sem.at[0, 1, v, h],
+                device_id=(count - 1,), device_id_type=mesh_id,
+            ).start()
 
     loads[vecs + 1].wait()
     values = [scalars[i] for i in range(energies.shape[0])]
@@ -257,6 +314,8 @@
         near = near + pltpu.roll(here, 1, 1) + pltpu.roll(here, lanes - 1, 1)
         for side in sides(k, h):
             part_copy(k, v, h, side).wait_recv()
+        if k + v + h == 0:
+            send_rest()
         if k < LANCZOS - 1:
             near = near + (halo[k, 0, v, at : at + rows] + halo[k, 1, v, at : at + rows])
         else:
@@ -289,10 +348,12 @@
     tile = jnp.zeros((vecs, 128), jnp.float32)
     turn = 0
     for i, (k, v, h) in enumerate(units):
-        if i == turn * GAP and turn <= rounds:
+        if i == turn * GAP + 1 and turn <= rounds:
             spread(turn)
             turn += 1
         unit(k, v, h)
+        if k == 1 and v * PARTS + h < DIRECT:
+            forward(v, h)
         if h == PARTS - 1:
             tile = gather(tile, k, v)
     while turn <= rounds:
@@ -319,6 +380,13 @@
         pltpu.make_async_copy(rest, rest, red_send.at[leg]).wait()
 
     exchange(0, near_part, member, RING, peer, tile)
+
+    @pl.when(is_relay == 1)
+    def _():
+        for v in range(vecs):
+            whole = halo.at[LANCZOS, 1, v, pl.ds(0, min(PARTS, DIRECT - v * PARTS) * rows)]
+            pltpu.make_async_copy(whole, whole, relay_sem.at[v]).wait()
+
     for side in range(2):
         whole = halo.at[pl.ds(0, LANCZOS - 1), 0]
         pltpu.make_async_copy(whole, whole, send_sem.at[side]).wait()
@@ -399,7 +467,7 @@
         out_specs=(vmem,) * 3,
         scratch_shapes=[
             pltpu.VMEM((LANCZOS, vecs, height + 2 * PAD, lanes), f32),
-            pltpu.VMEM((LANCZOS, 2, vecs, height, lanes), f32),
+            pltpu.VMEM((LANCZOS + 1, 2, vecs, height, lanes), f32),
             pltpu.VMEM((height, lanes), jnp.int32),
             pltpu.VMEM((height, lanes), f32),
             pltpu.VMEM((RING, vecs, 128), f32),

time: 73.5 us -> 71.8 us (0.977)
  Pallas kernels: 72.8 us -> 71.1 us
    pallas_call x1, Pallas kernels: 70.9 us -> 69.2 us  [shards(): pl.pallas_call(functools.partial(kernel, count), out_shape=(pltpu.VMEM((R...]
where the time goes in v4:
time: 71.8 us; the launch traced here: 71.7 us
  Pallas kernels  71.1 us (99%)
    pallas_call x1, Pallas kernels, shards(): pl.pallas_call(functools.partial(kernel, count), out_shape=(pltpu.VMEM((R...  69.2 us
    pallas_call x1, Pallas kernels, shards(): pl.pallas_call(finish, out_shape=(jax.ShapeDtypeStruct(start_vectors.shap...  1.84 us

profile of v4, /device:TPU:1, one launch (start us, length us, event | category | flops | bytes accessed | tf_op | source)
XLA Modules:
  0.0 71.7 jit_solution(903328138154505983)
XLA Ops:
  0.6 69.2 %shard_map.66 = (f32[4,2,256,256]{3,2,1,0:T(8,128)S(1)}, f32[32,2,128]{2,1,0:T(2,128)S(1)}, f32[2,128]{1,0:T(2,128)S(1)}) custom-call(f32[16]{0:T(128)} %energies.1, f32[2,1,256,256]{3,2,1,0:T(8,128)} %start.1, s32[1,256,256]{2,1,0:T(8,128)} %levels.1), custom_call_target="tpu_custom_call" | custom-call | tf_op jit(solution)/shard_map/pallas_call | solution.py:459
  69.9 1.8 %shard_map.67 = (f32[2,1,256,256]{3,2,1,0:T(8,128)}, f32[2,8]{1,0:T(2,128)}, f32[2,7]{1,0:T(2,128)}, f32[2,6]{1,0:T(2,128)}) custom-call(f32[4,2,256,256]{3,2,1,0:T(8,128)S(1)} %get-tuple-element.7.terms, f32[32,2,128]{2,1,0:T(2,128)S(1)} %get-tuple-element.8.parts, f32[2,128]{1,0:T(2,128)S(1)} %get-tuple-element.9.table), custom_call_target="tpu_custom_call" | custom-call | tf_op jit(solution)/shard_map/pallas_call | solution.py:481

commit v5 on v4

--- a/solution.py
+++ b/solution.py
@@ -9,12 +9,12 @@
 
 LANCZOS = 8
 RING = 16
-PARTS = 8
+PARTS = 16
 PAD = 8
 FAR = 64
 RETURNED = 4
-DIRECT = 13
-GAP = 12
+DIRECT = 26
+GAP = 24
 
 
 def two_sum(a, b):
@@ -28,9 +28,15 @@
     return s, b - (s - a)
 
 
-def add(x, y):
-    s, e = two_sum(x[0], y[0])
-    return quick(s, e + (x[1] + y[1]))
+def sum_up(items):
+    rest = []
+    while len(items) > 1:
+        pairs = [two_sum(x, y) for x, y in zip(items[::2], items[1::2])]
+        items = [s for s, _ in pairs]
+        rest.extend(e for _, e in pairs)
+    while len(rest) > 1:
+        rest = [x + y for x, y in zip(rest[::2], rest[1::2])] + rest[len(rest) // 2 * 2 :]
+    return items[0], rest[0]
 
 
 def wide(x):
@@ -335,17 +341,16 @@
         note(2 * k, v, here * here)
         note(2 * k + 1, v, here * new)
 
-    lane = lax.broadcasted_iota(jnp.int32, (vecs, 128), 1)
-    line = lax.broadcasted_iota(jnp.int32, (vecs, 128), 0)
+    lane = lax.broadcasted_iota(jnp.int32, (1, 128), 1)
 
     def gather(tile, k, v):
         for d in (2 * k, 2 * k + 1):
             whole = jnp.sum(jnp.sum(sums[d, v], axis=0, keepdims=True), axis=1, keepdims=True)
-            tile = jnp.where((lane == d) & (line == v), whole, tile)
+            tile = jnp.where(lane == 2 * LANCZOS * v + d, whole, tile)
         return tile
 
     units = [(k, v, h) for k in range(LANCZOS) for v in range(vecs) for h in range(PARTS)]
-    tile = jnp.zeros((vecs, 128), jnp.float32)
+    tile = jnp.zeros((1, 128), jnp.float32)
     turn = 0
     for i, (k, v, h) in enumerate(units):
         if i == turn * GAP + 1 and turn <= rounds:
@@ -393,10 +398,7 @@
         half = halo.at[0, 0, pl.ds(0, vecs), pl.ds(0, height // 2)]
         pltpu.make_async_copy(half, half, last_sem.at[side]).wait()
     arrived(0, near_part, RING)
-    pairs = [two_sum(near_part[i], near_part[i + 1]) for i in range(0, RING, 2)]
-    while len(pairs) > 1:
-        pairs = [add(x, y) for x, y in zip(pairs[::2], pairs[1::2])]
-    high, low = pairs[0]
+    high, low = sum_up([near_part[i] for i in range(RING)])
     tile = jnp.where(lane < FAR, high, pltpu.roll(low, FAR, 1))
     exchange(1, sums_out, ring, rings, far, tile)
     sent(0, near_part, RING)
@@ -408,13 +410,11 @@
 def finish(terms, parts, table, cheb, diag_out, offd_out, moments_out, result, diag_own, offd_own, moments_own, out_sem):
     _, vecs, height, lanes = terms.shape
     width, mean = table[0:1], table[1:2]
-    pairs = []
-    for i in range(parts.shape[0]):
-        both = parts[i]
-        pairs.append((both, pltpu.roll(both, FAR, 1)))
-    while len(pairs) > 1:
-        pairs = [add(x, y) for x, y in zip(pairs[::2], pairs[1::2])]
-    high, low = pairs[0]
+    both, rest = sum_up([parts[i] for i in range(parts.shape[0])])
+    high = jnp.concatenate([pltpu.roll(both, (128 - 2 * LANCZOS * v) % 128, 1) if v else both for v in range(vecs)], axis=0)
+    low = jnp.concatenate([pltpu.roll(both, FAR - 2 * LANCZOS * v, 1) for v in range(vecs)], axis=0)
+    rest = jnp.concatenate([pltpu.roll(rest, 128 - 2 * LANCZOS * v, 1) if v else rest for v in range(vecs)], axis=0)
+    high, low = quick(high, low + rest)
 
     def pick(x, d):
         return jnp.broadcast_to(x[:, d : d + 1], (vecs, 128))
@@ -460,7 +460,7 @@
         functools.partial(kernel, count),
         out_shape=(
             pltpu.VMEM((RETURNED, vecs, height, lanes), f32),
-            pltpu.VMEM((rings, vecs, 128), f32),
+            pltpu.VMEM((rings, 1, 128), f32),
             pltpu.VMEM((2, 128), f32),
         ),
         in_specs=[anywhere] * 3,
@@ -470,8 +470,8 @@
             pltpu.VMEM((LANCZOS + 1, 2, vecs, height, lanes), f32),
             pltpu.VMEM((height, lanes), jnp.int32),
             pltpu.VMEM((height, lanes), f32),
-            pltpu.VMEM((RING, vecs, 128), f32),
-            pltpu.VMEM((2, vecs, 128), f32),
+            pltpu.VMEM((RING, 1, 128), f32),
+            pltpu.VMEM((2, 1, 128), f32),
             pltpu.SMEM(energies.shape, f32),
         ],
         compiler_params=pltpu.CompilerParams(

time: 71.8 us -> 70.9 us (0.987)
  Pallas kernels: 71.1 us -> 70.2 us
    pallas_call x1, Pallas kernels: 69.2 us -> 68.4 us  [shards(): pl.pallas_call(functools.partial(kernel, count), out_shape=(pltpu.VMEM((R...]
where the time goes in v5:
time: 70.9 us; the launch traced here: 70.8 us
  Pallas kernels  70.2 us (99%)
    pallas_call x1, Pallas kernels, shards(): pl.pallas_call(functools.partial(kernel, count), out_shape=(pltpu.VMEM((R...  68.4 us
    pallas_call x1, Pallas kernels, shards(): pl.pallas_call(finish, out_shape=(jax.ShapeDtypeStruct(start_vectors.shap...  1.81 us

profile of v5, /device:TPU:1, one launch (start us, length us, event | category | flops | bytes accessed | tf_op | source)
XLA Modules:
  0.0 70.8 jit_solution(1535349706608340849)
XLA Ops:
  0.6 68.4 %shard_map.66 = (f32[4,2,256,256]{3,2,1,0:T(8,128)S(1)}, f32[32,1,128]{2,1,0:T(1,128)S(1)}, f32[2,128]{1,0:T(2,128)S(1)}) custom-call(f32[16]{0:T(128)} %energies.1, f32[2,1,256,256]{3,2,1,0:T(8,128)} %start.1, s32[1,256,256]{2,1,0:T(8,128)} %levels.1), custom_call_target="tpu_custom_call" | custom-call | tf_op jit(solution)/shard_map/pallas_call | solution.py:459
  69.0 1.8 %shard_map.67 = (f32[2,1,256,256]{3,2,1,0:T(8,128)}, f32[2,8]{1,0:T(2,128)}, f32[2,7]{1,0:T(2,128)}, f32[2,6]{1,0:T(2,128)}) custom-call(f32[4,2,256,256]{3,2,1,0:T(8,128)S(1)} %get-tuple-element.7.terms, f32[32,1,128]{2,1,0:T(1,128)S(1)} %get-tuple-element.8.parts, f32[2,128]{1,0:T(2,128)S(1)} %get-tuple-element.9.table), custom_call_target="tpu_custom_call" | custom-call | tf_op jit(solution)/shard_map/pallas_call | solution.py:481

commit v6 on v5

--- a/solution.py
+++ b/solution.py
@@ -13,7 +13,7 @@
 PAD = 8
 FAR = 64
 RETURNED = 4
-DIRECT = 26
+DIRECT = 24
 GAP = 24
 
 
@@ -201,10 +201,10 @@
         copy.start()
 
     def peer(i):
-        return base + lax.rem(member + i, RING)
+        return base + i
 
     def far(i):
-        return lax.rem(me + i * RING, count)
+        return i * RING + member
 
     rounds = (count // 2).bit_length() - 1
 
@@ -369,11 +369,11 @@
         mine[leg] = tile
         slots[index] = tile
 
-        for i in sorted(range(1, size), key=lambda i: abs(2 * i - size)):
+        for i in range(size - 1):
             pltpu.make_async_remote_copy(
                 src_ref=mine.at[leg], dst_ref=slots.at[index],
                 send_sem=red_send.at[leg], recv_sem=red_recv.at[leg],
-                device_id=(target(i),), device_id_type=mesh_id,
+                device_id=(target(i + (i + size - index) // size),), device_id_type=mesh_id,
             ).start()
 
     def arrived(leg, slots, size):

time: 70.9 us -> 70.9 us (level)
  no operation moved by 1% of the time
where the time goes in v6:
time: 70.9 us; the launch traced here: 70.7 us
  Pallas kernels  70.1 us (99%)
    pallas_call x1, Pallas kernels, shards(): pl.pallas_call(functools.partial(kernel, count), out_shape=(pltpu.VMEM((R...  68.3 us
    pallas_call x1, Pallas kernels, shards(): pl.pallas_call(finish, out_shape=(jax.ShapeDtypeStruct(start_vectors.shap...  1.81 us

profile of v6, /device:TPU:1, one launch (start us, length us, event | category | flops | bytes accessed | tf_op | source)
XLA Modules:
  0.0 70.7 jit_solution(15998054760816073105)
XLA Ops:
  0.6 68.3 %shard_map.66 = (f32[4,2,256,256]{3,2,1,0:T(8,128)S(1)}, f32[32,1,128]{2,1,0:T(1,128)S(1)}, f32[2,128]{1,0:T(2,128)S(1)}) custom-call(f32[16]{0:T(128)} %energies.1, f32[2,1,256,256]{3,2,1,0:T(8,128)} %start.1, s32[1,256,256]{2,1,0:T(8,128)} %levels.1), custom_call_target="tpu_custom_call" | custom-call | tf_op jit(solution)/shard_map/pallas_call | solution.py:459
  68.9 1.8 %shard_map.67 = (f32[2,1,256,256]{3,2,1,0:T(8,128)}, f32[2,8]{1,0:T(2,128)}, f32[2,7]{1,0:T(2,128)}, f32[2,6]{1,0:T(2,128)}) custom-call(f32[4,2,256,256]{3,2,1,0:T(8,128)S(1)} %get-tuple-element.7.terms, f32[32,1,128]{2,1,0:T(1,128)S(1)} %get-tuple-element.8.parts, f32[2,128]{1,0:T(2,128)S(1)} %get-tuple-element.9.table), custom_call_target="tpu_custom_call" | custom-call | tf_op jit(solution)/shard_map/pallas_call | solution.py:481
